TPU v7x, 32 devices: a whole 2x2x4 slice. The times are simulated.
32 devices in a mesh: row: 8 (over z, y), col: 4 (over x, core).
Axes of the slice: x: 2, y: 2, z: 4, core: 2. Of those that a mesh axis runs over, the one named last changes fastest.
Arguments:
- layer_input: bfloat16 [2048, 8192], P('row'), may hold values from -7 to 7
- gain: float32 [8192], replicated, may hold values from 0.5 to 6
- d_query: bfloat16 [2048, 4096], P('row', 'col'), may hold values from -6 to 6
- d_keyval: bfloat16 [2048, 2048], P('row', 'col'), may hold values from -6 to 6
- w_query: bfloat16 [8192, 4096], P('row', 'col'), may hold values from -0.0625 to 0.0625
- w_keyval: bfloat16 [8192, 2048], P('row', 'col'), may hold values from -1 to 1
- d_resid: bfloat16 [2048, 8192], P('row', 'col'), may hold values from -6 to 6
Outputs:
- d_input: bfloat16 [2048, 8192], P('row', 'col')
- grad_wq: bfloat16 [8192, 4096], P('row', 'col')
- grad_wkv: bfloat16 [8192, 2048], P('row', 'col')
- grad_gain: float32 [8192], P('col')
- grad_square_sum: float32 [], replicated
All inputs are finite; a program needn't handle non-finite values.
Results may differ from a plain program's by a relative error of at most 0.023.
Values may be sent and summed in bfloat16 or wider, within the bound.
A program may use at most 128 MiB of HBM per device.

v0:
```python
import math
import jax
import jax.numpy as jnp
from jax import lax
from jax.sharding import PartitionSpec as P

epsilon = 1e-05


def local(layer_input, gain, d_query, d_keyval, w_query, w_keyval, d_resid):
    inputs = layer_input.astype(jnp.float32)
    inv_rms = lax.rsqrt(jnp.mean(inputs * inputs, axis=1, keepdims=True) + epsilon)
    normed = (inputs * inv_rms * gain).astype(jnp.bfloat16)
    model_width = inputs.shape[1]
    local_tokens = inputs.shape[0]
    tokens_all = local_tokens * lax.axis_size("row")
    scaling = 1.0 / math.sqrt(tokens_all)
    weight_scale = 1.0 / math.sqrt(local_tokens)
    contract_cols = (((1,), (1,)), ((), ()))
    partial_value = lax.dot_general(
        d_query,
        lax.all_gather(w_query, "row", axis=0, tiled=True),
        contract_cols,
        preferred_element_type=jnp.float32,
    )
    partial_value = partial_value + lax.dot_general(
        d_keyval,
        lax.all_gather(w_keyval, "row", axis=0, tiled=True),
        contract_cols,
        preferred_element_type=jnp.float32,
    )
    rounded = lax.optimization_barrier(partial_value.astype(jnp.bfloat16)).astype(jnp.float32)
    feature_grad = lax.psum_scatter(
        rounded.astype(jnp.bfloat16), "col", scatter_dimension=1, tiled=True
    ).astype(jnp.float32)
    slice_width = feature_grad.shape[1]
    col_start = lax.axis_index("col") * slice_width
    input_part = lax.dynamic_slice_in_dim(inputs, col_start, slice_width, 1)
    gain_part = lax.dynamic_slice_in_dim(gain, col_start, slice_width, 0)
    weighted = gain_part * feature_grad
    token_dot = lax.psum(jnp.sum(weighted * input_part, axis=1, keepdims=True), "col")
    d_input = (
        d_resid.astype(jnp.float32)
        + inv_rms * weighted
        - input_part * inv_rms**3 * token_dot / model_width
    ).astype(jnp.bfloat16)
    gain_partial = jnp.sum(feature_grad * input_part * inv_rms, axis=0) * scaling
    cotangent = jnp.concatenate([d_query, d_keyval], axis=1)
    query_cols = d_query.shape[1]
    columns = lax.all_to_all(normed, "row", split_axis=1, concat_axis=0, tiled=True)
    all_cotangents = lax.all_gather(cotangent, "row", axis=0, tiled=True)
    groups = lax.axis_size("row")
    column_blocks = columns.reshape(groups, local_tokens, columns.shape[1])
    grad_blocks = all_cotangents.reshape(groups, local_tokens, all_cotangents.shape[1])
    blocks = (
        lax.dot_general(
            column_blocks,
            grad_blocks,
            (((1,), (1,)), ((0,), (0,))),
            preferred_element_type=jnp.float32,
        )
        * weight_scale
    )
    summed = jnp.sum(blocks.astype(jnp.bfloat16).astype(jnp.float32), axis=0)
    grad_wq = summed[:, :query_cols].astype(jnp.bfloat16)
    grad_wkv = summed[:, query_cols:].astype(jnp.bfloat16)
    query_f = grad_wq.astype(jnp.float32)
    keyval_f = grad_wkv.astype(jnp.float32)
    tile_square = jnp.sum(query_f * query_f) + jnp.sum(keyval_f * keyval_f)
    grad_gain = lax.psum(gain_partial, "row")
    leading = jnp.where(
        lax.axis_index("row") == 0, jnp.sum(grad_gain * grad_gain), jnp.float32(0.0)
    )
    grand_total = lax.psum(tile_square + leading, ("row", "col"))
    grad_square_sum = grand_total / jnp.float32(model_width)
    return (d_input, grad_wq, grad_wkv, grad_gain, grad_square_sum)


def solution(mesh):
    placed = (
        P("row", None),
        P(),
        P("row", "col"),
        P("row", "col"),
        P("row", "col"),
        P("row", "col"),
        P("row", "col"),
    )
    return jax.shard_map(
        local,
        mesh=mesh,
        in_specs=placed,
        out_specs=(P("row", "col"), P("row", "col"), P("row", "col"), P("col"), P()),
        check_vma=False,
    )
```

profile of v0, /device:TPU:12, one launch (start us, length us, event | category | flops | bytes accessed | tf_op | source)
XLA Modules:
  0.0 671.1 jit_solution(14180824158022452798)
XLA Ops:
  7.2 0.7 all-gather.6.cloned.1.call-update
  8.0 0.7 all-gather.4.cloned.1.call-update
  8.7 2.1 pad_maximum_fusion
  10.8 3.3 multiply_reduce_fusion
  14.1 0.2 copy-done
  14.2 3.2 multiply_convert_fusion.1
  17.4 6.5 copy.13
  23.9 6.4 all-to-all-start
  30.3 181.7 %all-gather.6.cloned.1.call-done = bf16[8192,512]{1,0:T(8,128)(2,1)} async-done(((bf16[1024,512]{1,0:T(8,128)(2,1)}), bf16[8192,512]{1,0:T(8,128)(2,1)}) %all-gather.6.cloned.1.call-update) | async-done | bytes 8388624 | tf_op jit(solution)/shard_map/all_gather | solution.py:28
  212.1 9.0 %fusion.11 = f32[256,8192]{1,0:T(8,128)} fusion(bf16[256,512]{1,0:T(8,128)(2,1)S(1)} %copy-done.2, bf16[8192,512]{1,0:T(8,128)(2,1)} %all-gather.6.cloned.1.call-done), kind=kOutput, calls=%fused_computation.24 | convolution fusion | flops 2147483648 | bytes 17039360 | tf_op jit(solution)/shard_map/dot_general | solution.py:26
  221.0 219.9 %all-gather.4.cloned.1.call-done = bf16[8192,1024]{1,0:T(8,128)(2,1)} async-done(((bf16[1024,1024]{1,0:T(8,128)(2,1)}), bf16[8192,1024]{1,0:T(8,128)(2,1)}) %all-gather.4.cloned.1.call-update) | async-done | bytes 16777232 | tf_op jit(solution)/shard_map/all_gather | solution.py:22
  440.9 12.4 %fusion = bf16[256,8192]{1,0:T(8,128)(2,1)} fusion(f32[256,8192]{1,0:T(8,128)} %fusion.11, bf16[256,1024]{1,0:T(8,128)(2,1)S(1)} %copy-done.1, bf16[8192,1024]{1,0:T(8,128)(2,1)} %all-gather.4.cloned.1.call-done), kind=kOutput, calls=%fused_computation.2 | convolution fusion | flops 4299161600 | bytes 29884416 | tf_op jit(solution)/shard_map/dot_general | solution.py:20
  453.4 6.7 convert_element_type.35
  460.0 81.3 %all-gather.8.cloned.1.call-done = bf16[2048,1536]{1,0:T(8,128)(2,1)} async-done(((bf16[256,1536]{1,0:T(8,128)(2,1)}), bf16[2048,1536]{1,0:T(8,128)(2,1)}) %all-gather.8.cloned.1.call-update) | async-done | bytes 6291472 | tf_op jit(solution)/shard_map/all_gather | solution.py:51
  541.3 10.9 %fusion.1 = bf16[1024,1536]{1,0:T(8,128)(2,1)S(1)} fusion(bf16[8,256,1536]{2,1,0:T(8,128)(2,1)} %bitcast.11, bf16[256,8,1024]{0,2,1:T(8,128)(2,1)} %all-to-all-done), kind=kOutput, calls=%fused_computation.5 | convolution fusion | flops 6478626816 | bytes 13631488 | tf_op jit(solution)/shard_map/dot_general | solution.py:56
  552.2 2.0 multiply_reduce_fusion.2
  554.3 2.9 multiply_reduce_fusion.1
  558.5 29.9 %reduce-scatter.2.cloned.1.call-done = bf16[256,2048]{1,0:T(8,128)(2,1)} async-done(((bf16[256,8192]{1,0:T(8,128)(2,1)}), bf16[256,2048]{1,0:T(8,128)(2,1)}) %reduce-scatter.2.cloned.1.call-update) | async-done | bytes 1048592 | tf_op jit(solution)/shard_map/reduce_scatter | solution.py:33
  588.4 2.6 fusion.10
  591.0 15.3 %psum.22 = f32[2048]{0:T(1024)S(1)} all-reduce(f32[2048]{0:T(1024)S(1)} %broadcast_multiply_fusion), channel_id=1, replica_groups=mesh['row'=8,'col'=4] {'row'}, use_global_device_ids=true, to_apply=%region_6.0 | all-reduce | flops 2048 | bytes 16384 | tf_op jit(solution)/shard_map/psum | solution.py:70
  606.3 0.6 multiply_reduce_fusion.3
  607.5 6.0 psum.21
  613.5 45.6 %psum.23 = f32[]{:T(128)} all-reduce(f32[]{:T(128)S(6)} %add.44), channel_id=1, replica_groups=mesh['row'=8,'col'=4] {'row','col'}, use_global_device_ids=true, to_apply=%region_10.11 | all-reduce | flops 1 | bytes 8 | tf_op jit(solution)/shard_map/psum | solution.py:74
  659.8 3.6 fusion.7
  (21 shorter events, 0.2 us)
Async XLA Ops:
  7.2 204.9 %all-gather.6.cloned.1.call-start = ((), (), s32[]{:S(2)}) async-start(), calls=%async_computation.3 | async-start | bytes 9437184 | tf_op jit(solution)/shard_map/all_gather | solution.py:28
  7.9 6.2 copy-start.4
  7.9 433.0 %all-gather.4.cloned.1.call-start = ((), (), s32[]{:S(2)}) async-start(), calls=%async_computation.2 | async-start | bytes 18874368 | tf_op jit(solution)/shard_map/all_gather | solution.py:22
  8.7 532.6 %all-gather.8.cloned.1.call-start = ((), (), s32[]{:S(2)}) async-start(), calls=%async_computation.5 | async-start | bytes 7077888 | tf_op jit(solution)/shard_map/all_gather | solution.py:51
  10.8 3.5 copy-start
  23.9 188.1 %copy-start.2 = (bf16[256,512]{1,0:T(8,128)(2,1)S(1)}, bf16[256,512]{1,0:T(8,128)(2,1)}, u32[]{:S(2)}) copy-start(bf16[256,512]{1,0:T(8,128)(2,1)} %param.10) | copy-start | bytes 786436
  23.9 436.1 %all-to-all-start = ((bf16[256,8,1024]{0,2,1:T(8,128)(2,1)}), bf16[256,8,1024]{0,2,1:T(8,128)(2,1)}, u32[]{:S(2)}, u32[]{:S(2)}) async-start(bf16[256,8,1024]{0,2,1:T(8,128)(2,1)} %bitcast.10), calls=%async_computation.1 | async-start | bytes 8388608 | tf_op jit(solution)/shard_map/all_to_all | solution.py:50
  30.3 410.6 %copy-start.1 = (bf16[256,1024]{1,0:T(8,128)(2,1)S(1)}, bf16[256,1024]{1,0:T(8,128)(2,1)}, u32[]{:S(2)}) copy-start(bf16[256,1024]{1,0:T(8,128)(2,1)} %param.9) | copy-start | bytes 1572868
  30.3 558.1 %reduce-scatter.2.cloned.1.call-start = ((), (), s32[]{:S(2)}) async-start(), calls=%async_computation.4 | async-start | bytes 5242880 | tf_op jit(solution)/shard_map/reduce_scatter | solution.py:33
  554.3 105.5 %copy-start.3 = (bf16[256,2048]{1,0:T(8,128)(2,1)S(1)}, bf16[256,2048]{1,0:T(8,128)(2,1)}, u32[]{:S(2)}) copy-start(bf16[256,2048]{1,0:T(8,128)(2,1)} %param.13) | copy-start | bytes 3145732
  606.3 57.1 %copy-start.5 = (f32[2048]{0:T(1024)}, f32[2048]{0:T(1024)S(1)}, u32[]{:S(2)}) copy-start(f32[2048]{0:T(1024)S(1)} %psum.22) | copy-start | bytes 24580
Sparse Core Ops, SparseCore 0:
  10.1 201.9 all-gather.5
  214.2 226.7 all-gather.3
  443.7 97.5 all-gather.7
  543.7 44.6 reduce-scatter.1
where the time goes:
time: 672 us; the launch traced here: 671 us
  waiting for transfers between devices  514 us (76%)
  blocking collectives  66.8 us (10%)
  matrix products  32.3 us (5%)
  other arithmetic  27 us (4%)
  between operations  17.6 us (3%)
    all_gather x1, waiting for transfers between devices, local(): lax.all_gather(w_query, 'row', axis=0, tiled=True)  220 us
    all_gather x1, waiting for transfers between devices, local(): lax.all_gather(w_keyval, 'row', axis=0, tiled=True)  182 us
    all_gather x1, waiting for transfers between devices, local(): all_cotangents = lax.all_gather(cotangent, 'row', axis=0, tiled=True)  81.3 us
    psum x1, blocking collectives, local(): grand_total = lax.psum(tile_square + leading, ('row', 'col'))  45.6 us
    reduce_scatter x1, waiting for transfers between devices, local(): lax.psum_scatter(rounded.astype(jnp.bfloat16), 'col', scatter_dimension=1...  29.9 us
    psum x1, blocking collectives, local(): grad_gain = lax.psum(gain_partial, 'row')  15.3 us
  transfers between devices with their start and end apart: 5, of which 4 were waited for; matrix products, arithmetic and copies ran while one was open for 9% of the time, Pallas kernels for 0%

commit v1 on v0

--- a/solution.py
+++ b/solution.py
@@ -71,7 +71,7 @@
     leading = jnp.where(
         lax.axis_index("row") == 0, jnp.sum(grad_gain * grad_gain), jnp.float32(0.0)
     )
-    grand_total = lax.psum(tile_square + leading, ("row", "col"))
+    grand_total = jnp.sum(lax.all_gather(tile_square + leading, ("row", "col")), axis=0)
     grad_square_sum = grand_total / jnp.float32(model_width)
     return (d_input, grad_wq, grad_wkv, grad_gain, grad_square_sum)
 

time: 672 us -> 672 us (level)
    psum x1 -> x0, blocking collectives: 45.6 us -> none  [local(): grand_total = lax.psum(tile_square + leading, ('row', 'col'))]
    unnamed x0 -> x1, blocking collectives: none -> 45.4 us
where the time goes in v1:
time: 672 us
  waiting for transfers between devices  514 us (76%)
  blocking collectives  66.6 us (10%)
  matrix products  32.3 us (5%)
  other arithmetic  27.6 us (4%)
  between operations  17.6 us (3%)
  local copies, waits for them, and re-layouts  6.81 us (1%)
    all_gather x1, waiting for transfers between devices, local(): lax.all_gather(w_query, 'row', axis=0, tiled=True)  220 us
    all_gather x1, waiting for transfers between devices, local(): lax.all_gather(w_keyval, 'row', axis=0, tiled=True)  182 us
    all_gather x1, waiting for transfers between devices, local(): all_cotangents = lax.all_gather(cotangent, 'row', axis=0, tiled=True)  81.3 us
    unnamed x1, blocking collectives  45.4 us
    reduce_scatter x1, waiting for transfers between devices, local(): lax.psum_scatter(rounded.astype(jnp.bfloat16), 'col', scatter_dimension=1...  29.9 us
    psum x1, blocking collectives, local(): grad_gain = lax.psum(gain_partial, 'row')  15.3 us
  transfers between devices with their start and end apart: 5, of which 4 were waited for; matrix products, arithmetic and copies ran while one was open for 9% of the time, Pallas kernels for 0%

profile of v1, /device:TPU:12, one launch (start us, length us, event | category | flops | bytes accessed | tf_op | source)
XLA Modules:
  0.0 671.6 jit_solution(4827487894507442577)
XLA Ops:
  7.2 0.7 all-gather.6.cloned.1.call-update
  8.0 0.7 all-gather.4.cloned.1.call-update
  8.7 2.1 pad_maximum_fusion
  10.8 3.3 multiply_reduce_fusion
  14.2 3.2 multiply_convert_fusion.1
  17.4 6.5 copy.13
  23.9 6.4 all-to-all-start
  30.3 181.7 %all-gather.6.cloned.1.call-done = bf16[8192,512]{1,0:T(8,128)(2,1)} async-done(((bf16[1024,512]{1,0:T(8,128)(2,1)}), bf16[8192,512]{1,0:T(8,128)(2,1)}) %all-gather.6.cloned.1.call-update) | async-done | bytes 8388624 | tf_op jit(solution)/shard_map/all_gather | solution.py:28
  212.1 9.0 %fusion.11 = f32[256,8192]{1,0:T(8,128)} fusion(bf16[256,512]{1,0:T(8,128)(2,1)S(1)} %copy-done.2, bf16[8192,512]{1,0:T(8,128)(2,1)} %all-gather.6.cloned.1.call-done), kind=kOutput, calls=%fused_computation.24 | convolution fusion | flops 2147483648 | bytes 17039360 | tf_op jit(solution)/shard_map/dot_general | solution.py:26
  221.0 219.9 %all-gather.4.cloned.1.call-done = bf16[8192,1024]{1,0:T(8,128)(2,1)} async-done(((bf16[1024,1024]{1,0:T(8,128)(2,1)}), bf16[8192,1024]{1,0:T(8,128)(2,1)}) %all-gather.4.cloned.1.call-update) | async-done | bytes 16777232 | tf_op jit(solution)/shard_map/all_gather | solution.py:22
  440.9 12.4 %fusion = bf16[256,8192]{1,0:T(8,128)(2,1)} fusion(f32[256,8192]{1,0:T(8,128)} %fusion.11, bf16[256,1024]{1,0:T(8,128)(2,1)S(1)} %copy-done.1, bf16[8192,1024]{1,0:T(8,128)(2,1)} %all-gather.4.cloned.1.call-done), kind=kOutput, calls=%fused_computation.2 | convolution fusion | flops 4299161600 | bytes 29884416 | tf_op jit(solution)/shard_map/dot_general | solution.py:20
  453.4 6.7 convert_element_type.35
  460.0 81.3 %all-gather.8.cloned.1.call-done = bf16[2048,1536]{1,0:T(8,128)(2,1)} async-done(((bf16[256,1536]{1,0:T(8,128)(2,1)}), bf16[2048,1536]{1,0:T(8,128)(2,1)}) %all-gather.8.cloned.1.call-update) | async-done | bytes 6291472 | tf_op jit(solution)/shard_map/all_gather | solution.py:51
  541.3 10.9 %fusion.1 = bf16[1024,1536]{1,0:T(8,128)(2,1)S(1)} fusion(bf16[8,256,1536]{2,1,0:T(8,128)(2,1)} %bitcast.12, bf16[256,8,1024]{0,2,1:T(8,128)(2,1)} %all-to-all-done), kind=kOutput, calls=%fused_computation.5 | convolution fusion | flops 6478626816 | bytes 13631488 | tf_op jit(solution)/shard_map/dot_general | solution.py:56
  552.2 2.0 multiply_reduce_fusion.2
  554.3 2.9 multiply_reduce_fusion.1
  558.5 29.9 %reduce-scatter.2.cloned.1.call-done = bf16[256,2048]{1,0:T(8,128)(2,1)} async-done(((bf16[256,8192]{1,0:T(8,128)(2,1)}), bf16[256,2048]{1,0:T(8,128)(2,1)}) %reduce-scatter.2.cloned.1.call-update) | async-done | bytes 1048592 | tf_op jit(solution)/shard_map/reduce_scatter | solution.py:33
  588.4 2.6 fusion.10
  591.0 15.3 %psum.15 = f32[2048]{0:T(1024)S(1)} all-reduce(f32[2048]{0:T(1024)S(1)} %broadcast_multiply_fusion), channel_id=1, replica_groups=mesh['row'=8,'col'=4] {'row'}, use_global_device_ids=true, to_apply=%region_6.0 | all-reduce | flops 2048 | bytes 16384 | tf_op jit(solution)/shard_map/psum | solution.py:70
  606.3 0.6 multiply_reduce_fusion.3
  607.6 5.9 psum.14
  613.6 45.4 %all-reduce = f32[32]{0:T(128)S(1)} all-reduce(f32[32]{0:T(128)S(1)} %dynamic-update-slice), channel_id=1, replica_groups=mesh['row'=8,'col'=4] {'row','col'}, use_global_device_ids=true, to_apply=%add | all-reduce | flops 32 | bytes 256
  659.0 0.6 reduce_sum.79
  660.2 3.6 fusion.7
  (24 shorter events, 0.5 us)
Async XLA Ops:
  7.2 204.9 %all-gather.6.cloned.1.call-start = ((), (), s32[]{:S(2)}) async-start(), calls=%async_computation.3 | async-start | bytes 9437184 | tf_op jit(solution)/shard_map/all_gather | solution.py:28
  7.9 6.2 copy-start.4
  7.9 433.0 %all-gather.4.cloned.1.call-start = ((), (), s32[]{:S(2)}) async-start(), calls=%async_computation.2 | async-start | bytes 18874368 | tf_op jit(solution)/shard_map/all_gather | solution.py:22
  8.7 532.6 %all-gather.8.cloned.1.call-start = ((), (), s32[]{:S(2)}) async-start(), calls=%async_computation.5 | async-start | bytes 7077888 | tf_op jit(solution)/shard_map/all_gather | solution.py:51
  10.8 3.5 copy-start
  23.9 188.1 %copy-start.2 = (bf16[256,512]{1,0:T(8,128)(2,1)S(1)}, bf16[256,512]{1,0:T(8,128)(2,1)}, u32[]{:S(2)}) copy-start(bf16[256,512]{1,0:T(8,128)(2,1)} %param.10) | copy-start | bytes 786436
  23.9 436.1 %all-to-all-start = ((bf16[256,8,1024]{0,2,1:T(8,128)(2,1)}), bf16[256,8,1024]{0,2,1:T(8,128)(2,1)}, u32[]{:S(2)}, u32[]{:S(2)}) async-start(bf16[256,8,1024]{0,2,1:T(8,128)(2,1)} %bitcast.11), calls=%async_computation.1 | async-start | bytes 8388608 | tf_op jit(solution)/shard_map/all_to_all | solution.py:50
  30.3 410.6 %copy-start.1 = (bf16[256,1024]{1,0:T(8,128)(2,1)S(1)}, bf16[256,1024]{1,0:T(8,128)(2,1)}, u32[]{:S(2)}) copy-start(bf16[256,1024]{1,0:T(8,128)(2,1)} %param.9) | copy-start | bytes 1572868
  30.3 558.1 %reduce-scatter.2.cloned.1.call-start = ((), (), s32[]{:S(2)}) async-start(), calls=%async_computation.4 | async-start | bytes 5242880 | tf_op jit(solution)/shard_map/reduce_scatter | solution.py:33
  554.3 106.0 %copy-start.3 = (bf16[256,2048]{1,0:T(8,128)(2,1)S(1)}, bf16[256,2048]{1,0:T(8,128)(2,1)}, u32[]{:S(2)}) copy-start(bf16[256,2048]{1,0:T(8,128)(2,1)} %param.13) | copy-start | bytes 3145732
  606.3 57.6 %copy-start.5 = (f32[2048]{0:T(1024)}, f32[2048]{0:T(1024)S(1)}, u32[]{:S(2)}) copy-start(f32[2048]{0:T(1024)S(1)} %psum.15) | copy-start | bytes 24580
Sparse Core Ops, SparseCore 0:
  10.1 201.9 all-gather.5
  214.2 226.7 all-gather.3
  443.7 97.5 all-gather.7
  543.7 44.6 reduce-scatter.1
